TPU v7x, 32 devices: a whole 2x2x4 slice. The times are simulated.
32 devices in a mesh: north: 8 (over y, x, core), deep: 4 (over z).
Axes of the slice: x: 2, y: 2, z: 4, core: 2. Of those that a mesh axis runs over, the one named last changes fastest.
Arguments:
- velocity: float32 [4, 128, 64, 256], P(None, None, 'north', 'deep'), may hold values from -6 to 6
- coupling: float32 [4, 4], replicated, may hold values from -4 to 4
- symbol_x: float32 [128], replicated, may hold values from 0.3 to 3
- symbol_y: float32 [64], replicated, may hold values from 0.3 to 3
- symbol_z: float32 [256], replicated, may hold values from 0.3 to 3
Outputs:
- spectrum: float32 [4, 128, 64, 256], P(None, 'north', 'deep')
All inputs are finite; a program needn't handle non-finite values.
Results may differ from a plain program's by a relative error of at most 0.00007.
Values sent between devices are 32-bit elements; how exact they have to be, the bound alone decides.
A program may use at most 128 MiB of HBM per device.

v0:
```python
import jax
import jax.numpy as jnp
from jax import lax
from jax.sharding import PartitionSpec as P


def basis_table(count):
    rank = jnp.arange(count)
    angle = (
        jnp.pi
        / (count + 1)
        * ((rank[:, None] + 1) * (rank[None, :] + 1) % (2 * count + 2)).astype(jnp.float32)
    )
    return jnp.sin(angle) * (2.0 / (count + 1)) ** 0.5


def along_dim(values, dim):
    moved = jnp.tensordot(
        values, basis_table(values.shape[dim]), axes=([dim], [0]), precision=lax.Precision.HIGHEST
    )
    return jnp.moveaxis(moved, -1, dim)


def on_device(velocity, coupling, symbol_x, symbol_y, symbol_z):
    part_values = velocity
    part_values = along_dim(part_values, 1)
    part_values = lax.all_to_all(part_values, "north", split_axis=1, concat_axis=2, tiled=True)
    part_values = along_dim(part_values, 2)
    block_values = part_values
    block_values = lax.all_to_all(block_values, "deep", split_axis=2, concat_axis=3, tiled=True)
    block_values = along_dim(block_values, 3)
    share_x = block_values.shape[1]
    part_x = lax.dynamic_slice_in_dim(symbol_x, lax.axis_index("north") * share_x, share_x)
    share_y = block_values.shape[2]
    part_y = lax.dynamic_slice_in_dim(symbol_y, lax.axis_index("deep") * share_y, share_y)
    symbol = part_x[:, None, None] + part_y[None, :, None] + symbol_z[None, None, :]
    weight_xyz = 1.0 / (1.0 + symbol)
    mixed_fields = jnp.einsum(
        "ab,bxyz->axyz", coupling, block_values, precision=lax.Precision.HIGHEST
    )
    block_values = weight_xyz * block_values + (1.0 - weight_xyz) * mixed_fields
    return block_values


def solution(mesh):
    placed = (P(None, None, "north", "deep"), P(), P(), P(), P())
    return jax.shard_map(
        on_device,
        mesh=mesh,
        in_specs=placed,
        out_specs=P(None, "north", "deep", None),
        check_vma=False,
    )
```

profile of v0, /device:TPU:2, one launch (start us, length us, event | category | flops | bytes accessed | tf_op | source)
XLA Modules:
  0.0 93.1 jit_solution(7834806281157115720)
XLA Ops:
  0.0 0.0 copy-start
  0.0 1.2 %copy-done = f32[4,128,8,64]{1,3,2,0:T(8,128)S(1)} copy-done((f32[4,128,8,64]{1,3,2,0:T(8,128)S(1)}, f32[4,128,8,64]{1,3,2,0:T(8,128)}, u32[]{:S(2)}) %copy-start) | copy-done | bytes 1048600
  1.2 2.3 %fusion.29 = f32[128,2048]{0,1} fusion(f32[128,2048]{0,1:T(8,128)S(1)} %bitcast.42, s32[128]{0:T(128)S(1)} %iota_add_fusion.2), kind=kOutput, calls=%fused_computation.32 | convolution fusion | flops 402817024 | bytes 2097664
  3.5 3.1 %copy.17 = f32[4,128,8,64]{3,2,0,1:T(8,128)S(1)} copy(f32[4,128,8,64]{1,3,2,0:T(8,128)} %bitcast.47) | data formatting | bytes 2097152 | tf_op jit(solution)/shard_map/transpose | solution.py:21
  6.6 2.1 %reshape.72 = f32[8,1,32768]{2,1,0:T(1,128)} reshape(f32[128,4,8,64]{3,2,1,0:T(8,128)S(1)} %bitcast.44) | data formatting | bytes 2097152
  8.7 4.3 %all-to-all-start = ((f32[8,1,32768]{2,1,0:T(1,128)}), f32[8,1,32768]{2,1,0:T(1,128)S(1)}, u32[]{:S(2)}, u32[]{:S(2)}) async-start(f32[8,1,32768]{2,1,0:T(1,128)} %reshape.72), calls=%async_computation | async-start | bytes 2097152 | tf_op jit(solution)/shard_map/all_to_all | solution.py:27
  12.9 13.9 %all-to-all-done = f32[8,1,32768]{2,1,0:T(1,128)S(1)} async-done(((f32[8,1,32768]{2,1,0:T(1,128)}), f32[8,1,32768]{2,1,0:T(1,128)S(1)}, u32[]{:S(2)}, u32[]{:S(2)}) %all-to-all-start) | async-done | bytes 1048608 | tf_op jit(solution)/shard_map/all_to_all | solution.py:27
  26.8 0.6 broadcast.101
  27.4 4.5 %reduce = f32[8,32768]{1,0:T(8,128)} reduce(f32[8,1,32768]{2,1,0:T(1,128)S(1)} %all-to-all-done, f32[]{:T(128)} %broadcast.101), dimensions={1}, to_apply=%all_to_all.26.reduce_sub_computation | reduce | bytes 2097156 | tf_op jit(solution)/shard_map/all_to_all | solution.py:27
  31.9 2.1 %reshape.73 = f32[128,4,8,64]{3,2,1,0:T(8,128)S(1)} reshape(f32[8,32768]{1,0:T(8,128)} %reduce) | data formatting | bytes 2097152
  33.9 4.8 %fusion.3 = f32[4,16,64,64]{2,3,1,0:T(8,128)} fusion(f32[4,16,8,8,64]{4,3,0,1,2:T(8,128)S(1)} %bitcast.43, s32[64]{0:T(128)S(1)} %iota_add_fusion.1), kind=kOutput, calls=%fused_computation.3 | convolution fusion | flops 201367552 | bytes 2097408 | tf_op jit(solution)/shard_map/dot_general | solution.py:18
  38.7 3.1 %copy.21 = f32[4,16,64,64]{3,1,0,2:T(8,128)S(1)} copy(f32[4,16,64,64]{2,3,1,0:T(8,128)} %fusion.3) | data formatting | bytes 2097152 | tf_op jit(solution)/shard_map/transpose | solution.py:21
  41.9 0.0 copy-start.4
  41.9 0.0 copy-start.5
  41.9 0.0 copy-start.3
  41.9 2.4 %reshape.74 = f32[4,1,65536]{2,1,0:T(1,128)} reshape(f32[64,4,16,64]{3,2,1,0:T(8,128)S(1)} %bitcast.45) | data formatting | bytes 2097152
  44.3 4.9 %all-to-all-start.1 = ((f32[4,1,65536]{2,1,0:T(1,128)}), f32[4,1,65536]{2,1,0:T(1,128)S(1)}, u32[]{:S(2)}, u32[]{:S(2)}) async-start(f32[4,1,65536]{2,1,0:T(1,128)} %reshape.74), calls=%async_computation.1 | async-start | bytes 2097152 | tf_op jit(solution)/shard_map/all_to_all | solution.py:30
  49.2 0.0 copy-done.4
  49.2 0.1 dynamic_slice.7
  49.2 0.0 copy-done.5
  49.2 0.1 dynamic_slice.6
  49.3 0.1 broadcast_add_fusion
  49.4 0.0 copy-done.3
  49.4 0.8 add_divide_fusion
  50.2 24.9 %all-to-all-done.1 = f32[4,1,65536]{2,1,0:T(1,128)S(1)} async-done(((f32[4,1,65536]{2,1,0:T(1,128)}), f32[4,1,65536]{2,1,0:T(1,128)S(1)}, u32[]{:S(2)}, u32[]{:S(2)}) %all-to-all-start.1) | async-done | bytes 1048608 | tf_op jit(solution)/shard_map/all_to_all | solution.py:30
  75.1 4.6 %reduce.1 = f32[4,65536]{1,0:T(4,128)} reduce(f32[4,1,65536]{2,1,0:T(1,128)S(1)} %all-to-all-done.1, f32[]{:T(128)} %broadcast.101), dimensions={1}, to_apply=%all_to_all.30.reduce_sub_computation | reduce | bytes 2097156 | tf_op jit(solution)/shard_map/all_to_all | solution.py:30
  79.7 2.2 %reshape.75 = f32[64,4,16,64]{3,2,1,0:T(8,128)S(1)} reshape(f32[4,65536]{1,0:T(4,128)} %reduce.1) | data formatting | bytes 2097152
  82.0 2.7 %copy.23 = f32[4,16,16,4,64]{4,3,2,1,0:T(4,128)} copy(f32[4,16,16,4,64]{4,1,0,2,3:T(8,128)S(1)} %bitcast.46) | data formatting | bytes 2097152 | tf_op jit(solution)/shard_map/all_to_all | solution.py:30
  84.7 0.0 copy-start.2
  84.7 2.5 %all_to_all.33 = f32[4,16,16,256]{3,2,1,0:T(8,128)S(1)} reshape(f32[4,16,16,4,64]{4,3,2,1,0:T(4,128)} %copy.23) | data formatting | bytes 2097152 | tf_op jit(solution)/shard_map/all_to_all | solution.py:30
  87.2 0.0 copy-start.1
  87.2 2.1 %fusion.13 = f32[4,16,16,256]{3,2,1,0:T(8,128)S(1)} fusion(f32[4,16,16,256]{3,2,1,0:T(8,128)S(1)} %all_to_all.33, s32[256]{0:T(256)S(1)} %iota_add_fusion), kind=kOutput, calls=%fused_computation.14 | convolution fusion | flops 805961728 | bytes 2098176 | tf_op jit(solution)/shard_map/dot_general | solution.py:18
  89.3 0.0 copy-done.2
  89.3 2.5 %fusion.6 = f32[16,16,256,4]{2,3,1,0:T(4,128)S(1)} fusion(f32[4,16,16,256]{3,2,1,0:T(8,128)S(1)} %fusion.13, f32[4,4]{1,0:T(4,128)S(1)} %copy-done.2), kind=kOutput, calls=%fused_computation.6 | convolution fusion | flops 12582912 | bytes 2097216 | tf_op jit(solution)/shard_map/ab,bxyz->axyz/dot_general | solution.py:38
  91.8 0.0 copy-done.1
  91.8 1.3 %bitcast_add_fusion = f32[4,16,16,256]{3,2,1,0:T(8,128)} fusion(f32[16,16,256,4]{2,3,1,0:T(4,128)S(1)} %fusion.6, f32[4,16,16,256]{3,2,1,0:T(8,128)S(1)} %fusion.13, f32[16,16,256]{2,1,0:T(8,128)S(1)} %copy-done.1, f32[16,16,256]{2,1,0:T(8,128)S(1)} %get-tuple-element.5), kind=kLoop, calls=%fused_computation.4 | loop fusion | flops 786432 | bytes 3670016 | tf_op jit(solution)/shard_map/add | solution.py:41
  (3 shorter events, 0.0 us)
Async XLA Ops:
  0.0 1.2 %copy-start = (f32[4,128,8,64]{1,3,2,0:T(8,128)S(1)}, f32[4,128,8,64]{1,3,2,0:T(8,128)}, u32[]{:S(2)}) copy-start(f32[4,128,8,64]{1,3,2,0:T(8,128)} %param.5) | copy-start | bytes 3145732
  8.7 18.1 %all-to-all-start = ((f32[8,1,32768]{2,1,0:T(1,128)}), f32[8,1,32768]{2,1,0:T(1,128)S(1)}, u32[]{:S(2)}, u32[]{:S(2)}) async-start(f32[8,1,32768]{2,1,0:T(1,128)} %reshape.72), calls=%async_computation | async-start | bytes 2097152 | tf_op jit(solution)/shard_map/all_to_all | solution.py:27
  41.9 7.3 %copy-start.4 = (f32[64]{0:T(128)S(1)}, f32[64]{0:T(128)}, u32[]{:S(2)}) copy-start(f32[64]{0:T(128)} %param.8) | copy-start | bytes 772
  41.9 7.4 %copy-start.5 = (f32[128]{0:T(128)S(1)}, f32[128]{0:T(128)}, u32[]{:S(2)}) copy-start(f32[128]{0:T(128)} %param.7) | copy-start | bytes 1540
  41.9 7.5 %copy-start.3 = (f32[256]{0:T(256)S(1)}, f32[256]{0:T(256)}, u32[]{:S(2)}) copy-start(f32[256]{0:T(256)} %param.9) | copy-start | bytes 3076
  44.3 30.8 %all-to-all-start.1 = ((f32[4,1,65536]{2,1,0:T(1,128)}), f32[4,1,65536]{2,1,0:T(1,128)S(1)}, u32[]{:S(2)}, u32[]{:S(2)}) async-start(f32[4,1,65536]{2,1,0:T(1,128)} %reshape.74), calls=%async_computation.1 | async-start | bytes 2097152 | tf_op jit(solution)/shard_map/all_to_all | solution.py:30
  84.7 4.6 %copy-start.2 = (f32[4,4]{1,0:T(4,128)S(1)}, f32[4,4]{1,0:T(4,128)}, u32[]{:S(2)}) copy-start(f32[4,4]{1,0:T(4,128)} %param.6) | copy-start | bytes 196
  87.2 4.6 %copy-start.1 = (f32[16,16,256]{2,1,0:T(8,128)S(1)}, f32[16,16,256]{2,1,0:T(8,128)}, u32[]{:S(2)}) copy-start(f32[16,16,256]{2,1,0:T(8,128)} %get-tuple-element.6) | copy-start | bytes 786436
where the time goes:
time: 93.5 us; the launch traced here: 93.1 us
  waiting for transfers between devices  38.8 us (41%)
  local copies, waits for them, and re-layouts  22.1 us (24%)
  matrix products  11.6 us (12%)
  other arithmetic  11.3 us (12%)
  starting transfers between devices  9.12 us (10%)
    all_to_all x1, waiting for transfers between devices, on_device(): lax.all_to_all(block_values, 'deep', split_axis=2, concat_axis=3, tiled=T...  24.9 us
    all_to_all x1, waiting for transfers between devices, on_device(): lax.all_to_all(part_values, 'north', split_axis=1, concat_axis=2, tiled=T...  13.9 us
    unnamed x16, local copies, waits for them, and re-layouts  10.1 us
    dot_general x2, matrix products, along_dim(): jnp.tensordot(values, basis_table(values.shape[dim]), axes=([dim], [0]),...  6.89 us
    transpose x2, local copies, waits for them, and re-layouts, along_dim(): return jnp.moveaxis(moved, -1, dim)  6.15 us
    all_to_all x2, local copies, waits for them, and re-layouts, on_device(): lax.all_to_all(block_values, 'deep', split_axis=2, concat_axis=3, tiled=T...  5.19 us
    all_to_all x1, starting transfers between devices, on_device(): lax.all_to_all(block_values, 'deep', split_axis=2, concat_axis=3, tiled=T...  4.87 us
    all_to_all x1, other arithmetic, on_device(): lax.all_to_all(block_values, 'deep', split_axis=2, concat_axis=3, tiled=T...  4.63 us
  transfers between devices with their start and end apart: 2, of which 2 were waited for; matrix products, arithmetic and copies ran while one was open for 1% of the time, Pallas kernels for 0%

commit v1 on v0

--- a/solution.py
+++ b/solution.py
@@ -24,7 +24,16 @@
 def on_device(velocity, coupling, symbol_x, symbol_y, symbol_z):
     part_values = velocity
     part_values = along_dim(part_values, 1)
-    part_values = lax.all_to_all(part_values, "north", split_axis=1, concat_axis=2, tiled=True)
+
+    def do_streams(xs):
+        answer = jax.lax.axis_size("north")
+        before = jnp.split(xs, answer, 1)
+        finding = jnp.stack(before)
+        odd = jax.lax.all_to_all(finding, "north", 0, 0)
+        m_next = jnp.concatenate(odd, 2)
+        return m_next
+
+    part_values = do_streams(part_values)
     part_values = along_dim(part_values, 2)
     block_values = part_values
     block_values = lax.all_to_all(block_values, "deep", split_axis=2, concat_axis=3, tiled=True)

time: 93.5 us -> 113 us (1.21)
  local copies, waits for them, and re-layouts: 22.1 us -> 42.6 us
    another operation x0 -> x10, local copies, waits for them, and re-layouts: none -> 19.5 us  [do_streams(): finding = jnp.stack(before)]
    unnamed x16 -> x29, local copies, waits for them, and re-layouts: 10.1 us -> 14.1 us
    transpose x2 -> x1, local copies, waits for them, and re-layouts: 6.15 us -> 3.1 us  [along_dim(): return jnp.moveaxis(moved, -1, dim)]
where the time goes in v1:
time: 113 us
  local copies, waits for them, and re-layouts  42.6 us (38%)
  waiting for transfers between devices  38.8 us (34%)
  other arithmetic  11.3 us (10%)
  matrix products  10.7 us (9%)
  starting transfers between devices  9.12 us (8%)
    all_to_all x1, waiting for transfers between devices, on_device(): lax.all_to_all(block_values, 'deep', split_axis=2, concat_axis=3, tiled=T...  24.9 us
    another operation x10, local copies, waits for them, and re-layouts, do_streams(): finding = jnp.stack(before)  19.5 us
    unnamed x29, local copies, waits for them, and re-layouts  14.1 us
    all_to_all x1, waiting for transfers between devices, do_streams(): odd = jax.lax.all_to_all(finding, 'north', 0, 0)  13.9 us
    dot_general x2, matrix products, along_dim(): jnp.tensordot(values, basis_table(values.shape[dim]), axes=([dim], [0]),...  6.89 us
    all_to_all x2, local copies, waits for them, and re-layouts, on_device(): lax.all_to_all(block_values, 'deep', split_axis=2, concat_axis=3, tiled=T...  5.19 us
    all_to_all x1, starting transfers between devices, on_device(): lax.all_to_all(block_values, 'deep', split_axis=2, concat_axis=3, tiled=T...  4.87 us
    all_to_all x1, other arithmetic, on_device(): lax.all_to_all(block_values, 'deep', split_axis=2, concat_axis=3, tiled=T...  4.64 us
  transfers between devices with their start and end apart: 2, of which 2 were waited for; matrix products, arithmetic and copies ran while one was open for 1% of the time, Pallas kernels for 0%

profile of v1, /device:TPU:2, one launch (start us, length us, event | category | flops | bytes accessed | tf_op | source)
XLA Modules:
  0.0 112.7 jit_solution(17592133481644340484)
XLA Ops:
  0.0 0.0 copy-start
  0.0 1.2 %copy-done = f32[4,128,8,64]{1,3,2,0:T(8,128)S(1)} copy-done((f32[4,128,8,64]{1,3,2,0:T(8,128)S(1)}, f32[4,128,8,64]{1,3,2,0:T(8,128)}, u32[]{:S(2)}) %copy-start) | copy-done | bytes 1048600
  1.2 1.3 %fusion.29 = f32[128,2048]{0,1:S(1)} fusion(f32[128,2048]{0,1:T(8,128)S(1)} %bitcast.55, s32[128]{0:T(128)S(1)} %iota_add_fusion.2), kind=kOutput, calls=%fused_computation.40 | convolution fusion | flops 402817024 | bytes 2097664
  2.6 4.7 %slice_bitcast_fusion = (f32[1,4,16,8,64]{2,4,3,1,0:T(8,128)}, f32[1,4,16,8,64]{2,4,3,1,0:T(8,128)}, f32[1,4,16,8,64]{2,4,3,1,0:T(8,128)}, f32[1,4,16,8,64]{2,4,...) fusion(f32[4,128,8,64]{1,3,2,0:T(8,128)S(1)} %bitcast.56), kind=kLoop, calls=%fused_computation.4 | loop fusion | bytes 2097152 | tf_op jit(solution)/shard_map/stack | solution.py:31
  7.2 1.6 %copy.22 = f32[1,4,16,8,64]{4,3,2,1,0:T(8,128)S(1)} copy(f32[1,4,16,8,64]{2,4,3,1,0:T(8,128)} %get-tuple-element.5) | data formatting | bytes 262144 | tf_op jit(solution)/shard_map/stack | solution.py:31
  8.8 2.3 %copy.21 = f32[1,4,16,8,64]{4,3,2,1,0:T(8,128)} copy(f32[1,4,16,8,64]{2,4,3,1,0:T(8,128)} %get-tuple-element.6) | data formatting | bytes 262144 | tf_op jit(solution)/shard_map/stack | solution.py:31
  11.0 2.2 %copy.20 = f32[1,4,16,8,64]{4,3,2,1,0:T(8,128)} copy(f32[1,4,16,8,64]{2,4,3,1,0:T(8,128)} %get-tuple-element.7) | data formatting | bytes 262144 | tf_op jit(solution)/shard_map/stack | solution.py:31
  13.3 2.3 %copy.19 = f32[1,4,16,8,64]{4,3,2,1,0:T(8,128)} copy(f32[1,4,16,8,64]{2,4,3,1,0:T(8,128)} %get-tuple-element.8) | data formatting | bytes 262144 | tf_op jit(solution)/shard_map/stack | solution.py:31
  15.5 2.3 %copy.18 = f32[1,4,16,8,64]{4,3,2,1,0:T(8,128)} copy(f32[1,4,16,8,64]{2,4,3,1,0:T(8,128)} %get-tuple-element.9) | data formatting | bytes 262144 | tf_op jit(solution)/shard_map/stack | solution.py:31
  17.8 2.2 %copy.17 = f32[1,4,16,8,64]{4,3,2,1,0:T(8,128)} copy(f32[1,4,16,8,64]{2,4,3,1,0:T(8,128)} %get-tuple-element.10) | data formatting | bytes 262144 | tf_op jit(solution)/shard_map/stack | solution.py:31
  20.0 1.0 copy.16
  21.1 1.0 copy.15
  22.1 0.0 copy-start.4
  22.1 0.0 copy-start.3
  22.1 0.0 copy-start.2
  22.1 1.0 constant_dynamic-update-slice_fusion.7
  23.1 1.0 constant_dynamic-update-slice_fusion.6
  24.1 1.0 constant_dynamic-update-slice_fusion.5
  25.1 1.0 constant_dynamic-update-slice_fusion.4
  26.1 0.0 copy-done.4
  26.1 0.0 copy-done.3
  26.1 0.0 copy-done.2
  26.2 2.1 %reshape.80 = f32[8,1,32768]{2,1,0:T(1,128)} reshape(f32[8,4,16,8,64]{4,3,2,1,0:T(8,128)S(1)} %constant_dynamic-update-slice_fusion) | data formatting | bytes 2097152
  28.3 4.3 %all-to-all-start = ((f32[8,1,32768]{2,1,0:T(1,128)}), f32[8,1,32768]{2,1,0:T(1,128)S(1)}, u32[]{:S(2)}, u32[]{:S(2)}) async-start(f32[8,1,32768]{2,1,0:T(1,128)} %reshape.80), calls=%async_computation | async-start | bytes 2097152 | tf_op jit(solution)/shard_map/all_to_all | solution.py:32
  32.6 13.9 %all-to-all-done = f32[8,1,32768]{2,1,0:T(1,128)S(1)} async-done(((f32[8,1,32768]{2,1,0:T(1,128)}), f32[8,1,32768]{2,1,0:T(1,128)S(1)}, u32[]{:S(2)}, u32[]{:S(2)}) %all-to-all-start) | async-done | bytes 1048608 | tf_op jit(solution)/shard_map/all_to_all | solution.py:32
  46.5 0.5 broadcast.101
  47.0 4.5 %reduce = f32[8,32768]{1,0:T(8,128)} reduce(f32[8,1,32768]{2,1,0:T(1,128)S(1)} %all-to-all-done, f32[]{:T(128)} %broadcast.101), dimensions={1}, to_apply=%all_to_all.16.reduce_sub_computation | reduce | bytes 2097156 | tf_op jit(solution)/shard_map/all_to_all | solution.py:32
  51.5 2.1 %reshape.81 = f32[8,4,16,8,64]{4,3,2,1,0:T(8,128)S(1)} reshape(f32[8,32768]{1,0:T(8,128)} %reduce) | data formatting | bytes 2097152
  53.5 4.8 %fusion.3 = f32[4,16,64,64]{2,3,1,0:T(8,128)} fusion(f32[8,4,16,8,64]{4,3,2,1,0:T(8,128)S(1)} %reshape.81, s32[64]{0:T(128)S(1)} %iota_add_fusion.1), kind=kOutput, calls=%fused_computation.3 | convolution fusion | flops 201367552 | bytes 2097408 | tf_op jit(solution)/shard_map/dot_general | solution.py:18
  58.4 3.1 %copy.25 = f32[4,16,64,64]{3,1,0,2:T(8,128)S(1)} copy(f32[4,16,64,64]{2,3,1,0:T(8,128)} %fusion.3) | data formatting | bytes 2097152 | tf_op jit(solution)/shard_map/transpose | solution.py:21
  61.5 0.0 copy-start.7
  61.5 0.0 copy-start.8
  61.5 0.0 copy-start.6
  61.5 2.4 %reshape.82 = f32[4,1,65536]{2,1,0:T(1,128)} reshape(f32[64,4,16,64]{3,2,1,0:T(8,128)S(1)} %bitcast.57) | data formatting | bytes 2097152
  63.9 4.9 %all-to-all-start.1 = ((f32[4,1,65536]{2,1,0:T(1,128)}), f32[4,1,65536]{2,1,0:T(1,128)S(1)}, u32[]{:S(2)}, u32[]{:S(2)}) async-start(f32[4,1,65536]{2,1,0:T(1,128)} %reshape.82), calls=%async_computation.1 | async-start | bytes 2097152 | tf_op jit(solution)/shard_map/all_to_all | solution.py:39
  68.8 0.0 copy-done.7
  68.8 0.1 dynamic_slice.7
  68.8 0.0 copy-done.8
  68.9 0.1 dynamic_slice.6
  68.9 0.1 broadcast_add_fusion
  69.0 0.0 copy-done.6
  69.0 0.8 add_divide_fusion
  69.8 24.9 %all-to-all-done.1 = f32[4,1,65536]{2,1,0:T(1,128)S(1)} async-done(((f32[4,1,65536]{2,1,0:T(1,128)}), f32[4,1,65536]{2,1,0:T(1,128)S(1)}, u32[]{:S(2)}, u32[]{:S(2)}) %all-to-all-start.1) | async-done | bytes 1048608 | tf_op jit(solution)/shard_map/all_to_all | solution.py:39
  94.7 4.6 %reduce.1 = f32[4,65536]{1,0:T(4,128)} reduce(f32[4,1,65536]{2,1,0:T(1,128)S(1)} %all-to-all-done.1, f32[]{:T(128)} %broadcast.101), dimensions={1}, to_apply=%all_to_all.17.reduce_sub_computation | reduce | bytes 2097156 | tf_op jit(solution)/shard_map/all_to_all | solution.py:39
  99.4 2.2 %reshape.83 = f32[64,4,16,64]{3,2,1,0:T(8,128)S(1)} reshape(f32[4,65536]{1,0:T(4,128)} %reduce.1) | data formatting | bytes 2097152
  101.6 2.7 %copy.27 = f32[4,16,16,4,64]{4,3,2,1,0:T(4,128)} copy(f32[4,16,16,4,64]{4,1,0,2,3:T(8,128)S(1)} %bitcast.58) | data formatting | bytes 2097152 | tf_op jit(solution)/shard_map/all_to_all | solution.py:39
  104.3 0.0 copy-start.5
  104.3 2.5 %all_to_all.20 = f32[4,16,16,256]{3,2,1,0:T(8,128)S(1)} reshape(f32[4,16,16,4,64]{4,3,2,1,0:T(4,128)} %copy.27) | data formatting | bytes 2097152 | tf_op jit(solution)/shard_map/all_to_all | solution.py:39
  106.8 0.0 copy-start.1
  106.8 2.1 %fusion.13 = f32[4,16,16,256]{3,2,1,0:T(8,128)S(1)} fusion(f32[4,16,16,256]{3,2,1,0:T(8,128)S(1)} %all_to_all.20, s32[256]{0:T(256)S(1)} %iota_add_fusion), kind=kOutput, calls=%fused_computation.22 | convolution fusion | flops 805961728 | bytes 2098176 | tf_op jit(solution)/shard_map/dot_general | solution.py:18
  108.9 0.0 copy-done.5
  108.9 2.5 %fusion.6 = f32[16,16,256,4]{2,3,1,0:T(4,128)S(1)} fusion(f32[4,16,16,256]{3,2,1,0:T(8,128)S(1)} %fusion.13, f32[4,4]{1,0:T(4,128)S(1)} %copy-done.5), kind=kOutput, calls=%fused_computation.14 | convolution fusion | flops 12582912 | bytes 2097216 | tf_op jit(solution)/shard_map/ab,bxyz->axyz/dot_general | solution.py:47
  111.4 0.0 copy-done.1
  111.4 1.3 %bitcast_add_fusion = f32[4,16,16,256]{3,2,1,0:T(8,128)} fusion(f32[16,16,256,4]{2,3,1,0:T(4,128)S(1)} %fusion.6, f32[4,16,16,256]{3,2,1,0:T(8,128)S(1)} %fusion.13, f32[16,16,256]{2,1,0:T(8,128)S(1)} %copy-done.1, f32[16,16,256]{2,1,0:T(8,128)S(1)} %get-tuple-element.13), kind=kLoop, calls=%fused_computation.12 | loop fusion | flops 786432 | bytes 3670016 | tf_op jit(solution)/shard_map/add | solution.py:50
  (7 shorter events, 0.1 us)
Async XLA Ops:
  0.0 1.2 %copy-start = (f32[4,128,8,64]{1,3,2,0:T(8,128)S(1)}, f32[4,128,8,64]{1,3,2,0:T(8,128)}, u32[]{:S(2)}) copy-start(f32[4,128,8,64]{1,3,2,0:T(8,128)} %param.5) | copy-start | bytes 3145732
  22.1 4.0 %copy-start.4 = (f32[1,4,16,8,64]{4,3,2,1,0:T(8,128)S(1)}, f32[1,4,16,8,64]{4,3,2,1,0:T(8,128)}, u32[]{:S(2)}) copy-start(f32[1,4,16,8,64]{4,3,2,1,0:T(8,128)} %copy.19) | copy-start | bytes 393220
  22.1 4.0 %copy-start.3 = (f32[1,4,16,8,64]{4,3,2,1,0:T(8,128)S(1)}, f32[1,4,16,8,64]{4,3,2,1,0:T(8,128)}, u32[]{:S(2)}) copy-start(f32[1,4,16,8,64]{4,3,2,1,0:T(8,128)} %copy.20) | copy-start | bytes 393220
  22.1 4.0 %copy-start.2 = (f32[1,4,16,8,64]{4,3,2,1,0:T(8,128)S(1)}, f32[1,4,16,8,64]{4,3,2,1,0:T(8,128)}, u32[]{:S(2)}) copy-start(f32[1,4,16,8,64]{4,3,2,1,0:T(8,128)} %copy.21) | copy-start | bytes 393220
  28.3 18.1 %all-to-all-start = ((f32[8,1,32768]{2,1,0:T(1,128)}), f32[8,1,32768]{2,1,0:T(1,128)S(1)}, u32[]{:S(2)}, u32[]{:S(2)}) async-start(f32[8,1,32768]{2,1,0:T(1,128)} %reshape.80), calls=%async_computation | async-start | bytes 2097152 | tf_op jit(solution)/shard_map/all_to_all | solution.py:32
  61.5 7.3 %copy-start.7 = (f32[64]{0:T(128)S(1)}, f32[64]{0:T(128)}, u32[]{:S(2)}) copy-start(f32[64]{0:T(128)} %param.8) | copy-start | bytes 772
  61.5 7.4 %copy-start.8 = (f32[128]{0:T(128)S(1)}, f32[128]{0:T(128)}, u32[]{:S(2)}) copy-start(f32[128]{0:T(128)} %param.7) | copy-start | bytes 1540
  61.5 7.5 %copy-start.6 = (f32[256]{0:T(256)S(1)}, f32[256]{0:T(256)}, u32[]{:S(2)}) copy-start(f32[256]{0:T(256)} %param.9) | copy-start | bytes 3076
  63.9 30.8 %all-to-all-start.1 = ((f32[4,1,65536]{2,1,0:T(1,128)}), f32[4,1,65536]{2,1,0:T(1,128)S(1)}, u32[]{:S(2)}, u32[]{:S(2)}) async-start(f32[4,1,65536]{2,1,0:T(1,128)} %reshape.82), calls=%async_computation.1 | async-start | bytes 2097152 | tf_op jit(solution)/shard_map/all_to_all | solution.py:39
  104.3 4.6 %copy-start.5 = (f32[4,4]{1,0:T(4,128)S(1)}, f32[4,4]{1,0:T(4,128)}, u32[]{:S(2)}) copy-start(f32[4,4]{1,0:T(4,128)} %param.6) | copy-start | bytes 196
  106.8 4.6 %copy-start.1 = (f32[16,16,256]{2,1,0:T(8,128)S(1)}, f32[16,16,256]{2,1,0:T(8,128)}, u32[]{:S(2)}) copy-start(f32[16,16,256]{2,1,0:T(8,128)} %get-tuple-element.14) | copy-start | bytes 786436
